TPU v7x, 256 devices: a whole 4x4x8 slice. The times are simulated.
256 devices in a mesh: gx: 32 (over y, z_lo, core), gy: 8 (over x, z_hi).
Axes of the slice: x: 4, y: 4, z: 8 (z_hi: 2, z_lo: 4; z = z_hi * 4 + z_lo), core: 2. Of those that a mesh axis runs over, the one named last changes fastest.
Arguments:
- signal: float32 [45, 32, 64, 128], P(None, 'gx', 'gy'), may hold values from -6 to 6
- response: float32 [45], replicated, may hold values from 0.2 to 2
- basis: float32 [362, 45], replicated, may hold values from -0.875 to 0.875
- mask: int32 [32, 64, 128], P('gx', 'gy'), may hold values 0 or 1
- coefficients: float32 [45, 32, 64, 128], P(None, 'gx', 'gy'), may hold values from -6 to 6
- extrapolated: float32 [45, 32, 64, 128], P(None, 'gx', 'gy'), may hold values from -6 to 6
- dual_grad: float32 [3, 362, 32, 64, 128], P(None, None, 'gx', 'gy'), may hold values from -2 to 2
- dual_sign: float32 [362, 32, 64, 128], P(None, 'gx', 'gy'), may hold values from -1 to 0
Outputs:
- coefficients_out: float32 [45, 32, 64, 128], P(None, 'gx', 'gy')
- extrapolated_out: float32 [45, 32, 64, 128], P(None, 'gx', 'gy')
- dual_grad_out: float32 [3, 362, 32, 64, 128], P(None, None, 'gx', 'gy')
- dual_sign_out: float32 [362, 32, 64, 128], P(None, 'gx', 'gy')
Inputs may be any that keep to these rules, and one draw needn't show every extreme that they name: `mask`: 1 marks a voxel inside the brain.
All inputs are finite; a program needn't handle non-finite values. No bound on the sum of `mask` on one device may be relied on, other than what follows from the above.
Results may differ from a plain program's by a relative error of at most 0.0001.
Values sent between devices are 32-bit elements; how exact they have to be, the bound alone decides.
A program may use at most 64 MiB of HBM per device.

v0:
```python
import jax
import jax.numpy as jnp
from jax import lax
from jax.sharding import PartitionSpec as P

ITERS = 2


STEP_PRIMAL = 0.25
STEP_DUAL = 0.02
TV_WEIGHT = 0.5


def from_behind(value, axis, steps):
    count = lax.axis_size(axis)
    leading, last = (max(0, -steps), min(count, count - steps))
    return lax.ppermute(value, axis, [(source, source + steps) for source in range(leading, last)])


def to_sphere(basis, coef_rows):
    count = coef_rows.shape[0]
    result = jnp.dot(
        basis,
        coef_rows.reshape(count, -1),
        precision=lax.Precision.HIGHEST,
        preferred_element_type=jnp.float32,
    )
    return result.reshape((basis.shape[0],) + coef_rows.shape[1:])


def to_harmonics(basis, amp_rows):
    count = amp_rows.shape[0]
    result = jnp.dot(
        basis.T,
        amp_rows.reshape(count, -1),
        precision=lax.Precision.HIGHEST,
        preferred_element_type=jnp.float32,
    )
    return result.reshape((basis.shape[1],) + amp_rows.shape[1:])


def forward_diff(field, along):
    length = field.shape[along]
    upper_part = lax.slice_in_dim(field, 1, length, axis=along)
    lower_part = lax.slice_in_dim(field, 0, length - 1, axis=along)
    zero_face = jnp.zeros_like(lax.slice_in_dim(field, 0, 1, axis=along))
    return jnp.concatenate([upper_part - lower_part, zero_face], along)


def backward_diff(dual_part, along):
    length = dual_part.shape[along]
    kept_rows = lax.slice_in_dim(dual_part, 0, length - 1, axis=along)
    zero_face = jnp.zeros_like(lax.slice_in_dim(dual_part, 0, 1, axis=along))
    masked = jnp.concatenate([kept_rows, zero_face], along)
    before = jnp.concatenate([zero_face, kept_rows], along)
    return masked - before


def keep_factor(field, is_last, along):
    length = field.shape[along]
    shape_now = [1] * field.ndim
    shape_now[along] = length
    position = lax.broadcasted_iota(jnp.int32, tuple(shape_now), along)
    dropped = jnp.logical_and(is_last, position == length - 1)
    return jnp.where(dropped, 0.0, 1.0).astype(jnp.float32)


def edge_diff(field, after_rows, is_last, along):
    length = field.shape[along]
    upper_part = jnp.concatenate(
        [lax.slice_in_dim(field, 1, length, axis=along), after_rows], along
    )
    return (upper_part - field) * keep_factor(field, is_last, along)


def zero_last(dual_part, is_last, along):
    return dual_part * keep_factor(dual_part, is_last, along)


def inner_div(masked, along):
    length = masked.shape[along]
    zero_face = jnp.zeros_like(lax.slice_in_dim(masked, 0, 1, axis=along))
    before = jnp.concatenate(
        [zero_face, lax.slice_in_dim(masked, 0, length - 1, axis=along)], along
    )
    return masked - before


def add_first(field, face_rows, along):
    length = field.shape[along]
    first_rows = lax.slice_in_dim(field, 0, 1, axis=along) + face_rows
    return jnp.concatenate([first_rows, lax.slice_in_dim(field, 1, length, axis=along)], along)


def last_face(field, along):
    length = field.shape[along]
    return lax.slice_in_dim(field, length - 1, length, axis=along)


def per_device(signal, response, basis, mask, coefficients, extrapolated, dual_grad, dual_sign):
    last_x = lax.axis_index("gx") == lax.axis_size("gx") - 1
    last_y = lax.axis_index("gy") == lax.axis_size("gy") - 1
    weight = mask.astype(jnp.float32)[None] * response[:, None, None, None]
    target = STEP_PRIMAL * weight * signal
    divisor = 1.0 + STEP_PRIMAL * weight * response[:, None, None, None]
    for iteration in range(ITERS):
        sphere_now = to_sphere(basis, extrapolated)
        after_x = to_sphere(basis, from_behind(extrapolated, "gx", -1))
        after_y = to_sphere(basis, from_behind(extrapolated[:, :, :1], "gy", -1))
        stepped_x = dual_grad[0] + STEP_DUAL * edge_diff(sphere_now, after_x, last_x, 1)
        stepped_y = dual_grad[1] + STEP_DUAL * edge_diff(sphere_now, after_y, last_y, 2)
        stepped_z = dual_grad[2] + STEP_DUAL * forward_diff(sphere_now, 3)
        magnitude = jnp.sqrt(stepped_x * stepped_x + stepped_y * stepped_y + stepped_z * stepped_z)
        shrink = jnp.maximum(1.0, magnitude / TV_WEIGHT)
        dual_grad = jnp.stack([stepped_x / shrink, stepped_y / shrink, stepped_z / shrink])
        dual_sign = jnp.minimum(0.0, dual_sign + STEP_DUAL * sphere_now)
        masked_x = zero_last(dual_grad[0], last_x, 1)
        masked_y = zero_last(dual_grad[1], last_y, 2)
        backward = dual_sign - (
            inner_div(masked_x, 1) + inner_div(masked_y, 2) + backward_diff(dual_grad[2], 3)
        )
        harmonic = to_harmonics(basis, backward)
        before_x = from_behind(to_harmonics(basis, last_face(masked_x, 1)), "gx", 1)
        before_y = from_behind(to_harmonics(basis, last_face(masked_y, 2)), "gy", 1)
        harmonic = add_first(add_first(harmonic, before_x, 1), before_y, 2)
        trial_step = coefficients - STEP_PRIMAL * harmonic
        updated = (trial_step + target) / divisor
        extrapolated = 2.0 * updated - coefficients
        coefficients = updated
    return (coefficients, extrapolated, dual_grad, dual_sign)


def solution(mesh):
    in_specs = (
        P(None, "gx", "gy", None),
        P(),
        P(),
        P("gx", "gy", None),
        P(None, "gx", "gy", None),
        P(None, "gx", "gy", None),
        P(None, None, "gx", "gy", None),
        P(None, "gx", "gy", None),
    )
    out_specs = (
        P(None, "gx", "gy", None),
        P(None, "gx", "gy", None),
        P(None, None, "gx", "gy", None),
        P(None, "gx", "gy", None),
    )
    return jax.shard_map(
        per_device, mesh=mesh, in_specs=in_specs, out_specs=out_specs, check_vma=False
    )
```

profile of v0, /device:TPU:26, one launch (start us, length us, event | category | flops | bytes accessed | tf_op | source)
XLA Modules:
  0.0 97.1 jit_solution(12035083772551387770)
XLA Ops:
  0.6 6.3 %collective-permute-start = (f32[45,1,8,128]{3,2,1,0:T(8,128)}, f32[45,1,8,128]{3,2,1,0:T(8,128)S(1)}, u32[]{:S(2)}, u32[]{:S(2)}) collective-permute-start(f32[45,1,8,128]{3,2,1,0:T(8,128)} %param.13), channel_id=1, source_target_pairs={{8,0},{16,8},{24,16},{32,24},{40,32},{48,40},{56,48},{64,56},{72,6... | collective-permute-start | bytes 552968 | tf_op jit(solution)/shard_map/ppermute | solution.py:17
  6.9 0.9 slice.68
  7.9 6.4 %collective-permute-start.1 = (f32[45,1,1,128]{3,0,2,1:T(8,128)S(1)}, f32[45,1,1,128]{3,0,2,1:T(8,128)S(1)}, u32[]{:S(2)}, u32[]{:S(2)}) collective-permute-start(f32[45,1,1,128]{3,0,2,1:T(8,128)S(1)} %copy.71), channel_id=1, source_target_pairs={{1,0},{2,1},{3,2},{4,3},{5,4},{6,5},{7,6},{9,8},{10,9},{11,10},{12... | collective-permute-start | bytes 69128 | tf_op jit(solution)/shard_map/ppermute | solution.py:17
  14.3 0.9 pad.21
  15.3 1.4 %fusion.46 = f32[362,1024]{1,0:T(8,128)S(1)} fusion(f32[362,45]{0,1:T(8,128)S(1)} %copy-done, f32[45,1024]{1,0:T(8,128)S(1)} %bitcast.227), kind=kOutput, calls=%fused_computation.95 | convolution fusion | flops 200171520 | bytes 1732232 | tf_op jit(solution)/shard_map/dot_general | solution.py:22
  17.0 1.3 %fusion.45 = (f32[362,8,128]{2,1,0:T(8,128)}, f32[362,1,8,128]{3,2,0,1:T(8,128)S(1)}) fusion(f32[368,8,128]{2,1,0:T(8,128)S(1)} %bitcast.220), kind=kLoop, calls=%fused_computation.94 | loop fusion | bytes 4448256
  19.1 1.7 %slice_bitcast_fusion.11 = (f32[362,7,128]{2,0,1:T(8,128)}, f32[362,1,7,128]{3,0,2,1:T(8,128)}) fusion(f32[362,1,8,128]{3,0,2,1:T(8,128)S(1)} %copy.32), kind=kLoop, calls=%fused_computation.89 | loop fusion | bytes 3892224 | tf_op jit(solution)/shard_map/concatenate | solution.py:70
  20.8 4.4 %fusion.44 = (f32[1,362,1,8,128]{4,3,2,1,0:T(8,128)}, f32[1,362,1,8,128]{4,3,2,1,0:T(8,128)}, f32[1,362,1,8,128]{4,3,2,1,0:T(8,128)}) fusion(f32[3,362,1,8,128]{4,3,2,1,0:T(8,128)} %param.14), kind=kLoop, calls=%fused_computation.93 | loop fusion | bytes 8896512 | tf_op jit(solution)/shard_map/slice | solution.py:110
  25.8 6.8 %broadcast_multiply_fusion.1 = (f32[362,1,8,128]{3,0,2,1:T(8,128)S(1)}, f32[362,1,8,128]{3,0,2,1:T(8,128)S(1)}, f32[362,1,8,128]{3,0,2,1:T(8,128)S(1)}, f32[362,8,128]{2,0,1:T(8,128)S(1)}) fusion(f32[8]{0:T(128)S(1)} %and_select_fusion, f32[362,1,8,128]{3,2,0,1:T(8,128)S(1)} %get-tuple-element.37, f32[362,1,1,128]{3,0,2,1:T(8,128)S(1)} %bitcast.225, ...), kind=kOutput, calls=%fused_computation.49 | convolution fusion | flops 209438720 | bytes 18030956 | tf_op jit(solution)/shard_map/dot_general | solution.py:22
  32.9 1.0 %copy-done.2 = f32[1,362,1,8,128]{4,3,2,1,0:T(8,128)S(1)} copy-done((f32[1,362,1,8,128]{4,3,2,1,0:T(8,128)S(1)}, f32[1,362,1,8,128]{4,3,2,1,0:T(8,128)}, u32[]{:S(2)}) %copy-start.2) | copy-done | bytes 1482776
  34.5 3.4 %collective-permute-start.3 = (f32[45,1,1,128]{3,0,2,1:T(8,128)S(1)}, f32[45,1,1,128]{3,0,2,1:T(8,128)S(1)}, u32[]{:S(2)}, u32[]{:S(2)}) collective-permute-start(f32[45,1,1,128]{3,0,2,1:T(8,128)S(1)} %convolution_bitcast_fusion.2), channel_id=1, source_target_pairs={{0,1},{1,2},{2,3},{3,4},{4,5},{5,6},{6,7},{8,9},{9,10},{10,11},{11... | collective-permute-start | bytes 69128 | tf_op jit(solution)/shard_map/ppermute | solution.py:17
  37.9 1.4 %add_subtract_fusion.1 = (f32[362,1,8,128]{3,0,2,1:T(8,128)S(1)}, f32[362,1,8,128]{3,0,2,1:T(8,128)S(1)}) fusion(f32[362,1,8,127]{3,0,2,1:T(8,128)S(1)} %bitcast.206, f32[362,1,8,128]{3,0,2,1:T(8,128)S(1)} %fusion.24, f32[362,1,8,128]{3,0,2,1:T(8,128)S(1)} %get-tuple-element.25, f32[362,1,7,128]{3,0,2,1:T(8,128)S(1)} %slice.89, ...), kind=kLoop, calls=%fused_computation.38 | loop fusion | flops 4077568 | bytes 14630724 | tf_op jit(solution)/shard_map/sub | solution.py:119
  39.2 0.9 copy_bitcast_fusion.4
  40.6 1.1 %fusion.48 = f32[1024,45]{0,1:T(8,128)S(1)} fusion(f32[362,1024]{1,0:T(8,128)S(1)} %bitcast.212, f32[362,45]{0,1:T(8,128)S(1)} %copy-done), kind=kOutput, calls=%fused_computation.97 | convolution fusion | flops 200171520 | bytes 1732232 | tf_op jit(solution)/shard_map/dot_general | solution.py:33
  41.8 2.1 %collective-permute-start.2 = (f32[45,1,8,128]{3,0,2,1:T(8,128)S(1)}, f32[45,1,8,128]{3,0,2,1:T(8,128)S(1)}, u32[]{:S(2)}, u32[]{:S(2)}) collective-permute-start(f32[45,1,8,128]{3,0,2,1:T(8,128)S(1)} %copy.47), channel_id=1, source_target_pairs={{0,8},{8,16},{16,24},{24,32},{32,40},{40,48},{48,56},{56,64},{64,7... | collective-permute-start | bytes 552968 | tf_op jit(solution)/shard_map/ppermute | solution.py:17
  44.4 1.1 %fusion.47 = f32[1024,45]{0,1:T(8,128)S(1)} fusion(f32[362,1024]{1,0:T(8,128)S(1)} %bitcast.214, f32[362,45]{0,1:T(8,128)S(1)} %copy-done), kind=kOutput, calls=%fused_computation.96 | convolution fusion | flops 200171520 | bytes 1732232 | tf_op jit(solution)/shard_map/dot_general | solution.py:33
  45.6 5.9 %collective-permute-done.2 = f32[45,1,8,128]{3,0,2,1:T(8,128)S(1)} collective-permute-done((f32[45,1,8,128]{3,0,2,1:T(8,128)S(1)}, f32[45,1,8,128]{3,0,2,1:T(8,128)S(1)}, u32[]{:S(2)}, u32[]{:S(2)}) %collective-permute-start.2) | collective-permute-done | bytes 184352 | tf_op jit(solution)/shard_map/ppermute | solution.py:17
  51.9 1.9 %collective-permute-start.4 = (f32[45,1,8,128]{3,0,2,1:T(8,128)S(1)}, f32[45,1,8,128]{3,0,2,1:T(8,128)S(1)}, u32[]{:S(2)}, u32[]{:S(2)}) collective-permute-start(f32[45,1,8,128]{3,0,2,1:T(8,128)S(1)} %get-tuple-element.21), channel_id=1, source_target_pairs={{8,0},{16,8},{24,16},{32,24},{40,32},{48,40},{56,48},{64,56},{72,6... | collective-permute-start | bytes 552968 | tf_op jit(solution)/shard_map/ppermute | solution.py:17
  53.8 7.3 %collective-permute-start.5 = (f32[45,1,1,128]{3,0,2,1:T(8,128)S(1)}, f32[45,1,1,128]{3,0,2,1:T(8,128)S(1)}, u32[]{:S(2)}, u32[]{:S(2)}) collective-permute-start(f32[45,1,1,128]{3,0,2,1:T(8,128)S(1)} %slice.95), channel_id=1, source_target_pairs={{1,0},{2,1},{3,2},{4,3},{5,4},{6,5},{7,6},{9,8},{10,9},{11,10},{12... | collective-permute-start | bytes 69128 | tf_op jit(solution)/shard_map/ppermute | solution.py:17
  61.2 1.4 %fusion.49 = f32[1024,362]{0,1:T(8,128)S(1)} fusion(f32[45,1024]{1,0:T(8,128)S(1)} %bitcast.230, f32[362,45]{0,1:T(8,128)S(1)} %copy-done), kind=kOutput, calls=%fused_computation.98 | convolution fusion | flops 200171520 | bytes 1732232 | tf_op jit(solution)/shard_map/dot_general | solution.py:22
  65.0 1.4 %fusion.50 = f32[1024,362]{0,1:T(8,128)S(1)} fusion(f32[45,1024]{1,0:T(8,128)S(1)} %bitcast.231, f32[362,45]{0,1:T(8,128)S(1)} %copy-done), kind=kOutput, calls=%fused_computation.99 | convolution fusion | flops 200171520 | bytes 1732232 | tf_op jit(solution)/shard_map/dot_general | solution.py:22
  66.9 1.2 %slice-done = f32[362,1,7,128]{3,0,2,1:T(8,128)S(1)} async-done(((f32[362,1,8,128]{3,0,2,1:T(8,128)}), f32[362,1,7,128]{3,0,2,1:T(8,128)S(1)}, s32[]{:S(2)}) %slice-start) | async-done | bytes 1297432 | tf_op jit(solution)/shard_map/slice | solution.py:71
  68.1 1.7 %divide_bitcast_fusion.1 = (f32[1,362,1,8,128]{4,1,3,2,0:T(8,128)S(1)}, f32[362,1,8,128]{3,0,2,1:T(8,128)S(1)}, f32[362,1,8,128]{3,0,2,1:T(8,128)S(1)}, f32[362,1,8,128]{3,0,2,1:T(8,128)S(1)}) fusion(f32[362,1,8,128]{3,0,2,1:T(8,128)S(1)} %fusion.24, f32[362,1,8,127]{3,0,2,1:T(8,128)S(1)} %slice_subtract_fusion, ...), kind=kLoop, calls=%fused_computation.92 | loop fusion | flops 7413760 | bytes 17781476 | tf_op jit(solution)/shard_map/stack | solution.py:115
  70.6 7.6 %collective-permute-start.7 = (f32[45,1,1,128]{3,0,2,1:T(8,128)S(1)}, f32[45,1,1,128]{3,0,2,1:T(8,128)S(1)}, u32[]{:S(2)}, u32[]{:S(2)}) collective-permute-start(f32[45,1,1,128]{3,0,2,1:T(8,128)S(1)} %convolution_bitcast_fusion.1), channel_id=1, source_target_pairs={{0,1},{1,2},{2,3},{3,4},{4,5},{5,6},{6,7},{8,9},{9,10},{10,11},{11... | collective-permute-start | bytes 69128 | tf_op jit(solution)/shard_map/ppermute | solution.py:17
  78.2 1.7 %add_subtract_fusion = (f32[362,1,8,128]{3,0,2,1:T(8,128)S(1)}, f32[362,1,8,128]{3,0,2,1:T(8,128)S(1)}, f32[362,1,8,128]{3,0,2,1:T(8,128)S(1)}) fusion(f32[362,1,8,127]{3,0,2,1:T(8,128)S(1)} %bitcast.207, f32[362,1,8,128]{3,0,2,1:T(8,128)S(1)} %get-tuple-element.33, f32[362,1,8,128]{3,0,2,1:T(8,128)S(1)} %get-tuple-element.32, ...), kind=kLoop, calls=%fused_computation.34 | loop fusion | flops 5189632 | bytes 17596228 | tf_op jit(solution)/shard_map/sub | solution.py:119
  80.8 1.1 %fusion.51 = f32[1024,45]{0,1:T(8,128)S(1)} fusion(f32[362,1024]{1,0:T(8,128)S(1)} %bitcast.218, f32[362,45]{0,1:T(8,128)S(1)} %copy-done), kind=kOutput, calls=%fused_computation.100 | convolution fusion | flops 200171520 | bytes 1732232 | tf_op jit(solution)/shard_map/dot_general | solution.py:33
  81.9 1.6 %copy.68 = f32[362,1,8,128]{3,2,1,0:T(8,128)} copy(f32[362,1,8,128]{3,0,2,1:T(8,128)S(1)} %get-tuple-element.19) | data formatting | bytes 2965504
  84.4 1.1 %fusion.52 = f32[1024,45]{0,1:T(8,128)S(1)} fusion(f32[362,1024]{1,0:T(8,128)S(1)} %bitcast.219, f32[362,45]{0,1:T(8,128)S(1)} %copy-done), kind=kOutput, calls=%fused_computation.101 | convolution fusion | flops 200171520 | bytes 1732232 | tf_op jit(solution)/shard_map/dot_general | solution.py:33
  85.7 1.9 %collective-permute-start.6 = (f32[45,1,8,128]{3,0,2,1:T(8,128)S(1)}, f32[45,1,8,128]{3,0,2,1:T(8,128)S(1)}, u32[]{:S(2)}, u32[]{:S(2)}) collective-permute-start(f32[45,1,8,128]{3,0,2,1:T(8,128)S(1)} %copy.63), channel_id=1, source_target_pairs={{0,8},{8,16},{16,24},{24,32},{32,40},{40,48},{48,56},{56,64},{64,7... | collective-permute-start | bytes 552968 | tf_op jit(solution)/shard_map/ppermute | solution.py:17
  88.1 3.4 %copy.67 = f32[3,362,1,8,128]{4,3,2,1,0:T(8,128)} copy(f32[3,362,1,8,128]{4,1,3,2,0:T(8,128)S(1)} %pad_maximum_fusion) | data formatting | bytes 8896512
  91.5 3.8 %collective-permute-done.6 = f32[45,1,8,128]{3,0,2,1:T(8,128)S(1)} collective-permute-done((f32[45,1,8,128]{3,0,2,1:T(8,128)S(1)}, f32[45,1,8,128]{3,0,2,1:T(8,128)S(1)}, u32[]{:S(2)}, u32[]{:S(2)}) %collective-permute-start.6) | collective-permute-done | bytes 184352 | tf_op jit(solution)/shard_map/ppermute | solution.py:17
  95.6 0.7 copy.66
  (86 shorter events, 10.9 us)
Async XLA Ops:
  0.6 14.6 %copy-start = (f32[362,45]{0,1:T(8,128)S(1)}, f32[362,45]{0,1:T(8,128)}, u32[]{:S(2)}) copy-start(f32[362,45]{0,1:T(8,128)} %param.10) | copy-start | bytes 195484
  0.6 25.1 %collective-permute-start = (f32[45,1,8,128]{3,2,1,0:T(8,128)}, f32[45,1,8,128]{3,2,1,0:T(8,128)S(1)}, u32[]{:S(2)}, u32[]{:S(2)}) collective-permute-start(f32[45,1,8,128]{3,2,1,0:T(8,128)} %param.13), channel_id=1, source_target_pairs={{8,0},{16,8},{24,16},{32,24},{40,32},{48,40},{56,48},{64,56},{72,6... | collective-permute-start | bytes 552968 | tf_op jit(solution)/shard_map/ppermute | solution.py:17
  7.9 17.4 %collective-permute-start.1 = (f32[45,1,1,128]{3,0,2,1:T(8,128)S(1)}, f32[45,1,1,128]{3,0,2,1:T(8,128)S(1)}, u32[]{:S(2)}, u32[]{:S(2)}) collective-permute-start(f32[45,1,1,128]{3,0,2,1:T(8,128)S(1)} %copy.71), channel_id=1, source_target_pairs={{1,0},{2,1},{3,2},{4,3},{5,4},{6,5},{7,6},{9,8},{10,9},{11,10},{12... | collective-permute-start | bytes 69128 | tf_op jit(solution)/shard_map/ppermute | solution.py:17
  19.1 1.7 %copy-start.8 = (f32[45]{0:T(128)S(1)}, f32[45]{0:T(128)}, u32[]{:S(2)}) copy-start(f32[45]{0:T(128)} %param.9) | copy-start | bytes 544
  19.1 1.7 %copy-start.7 = (s32[1,8,128]{2,1,0:T(8,128)S(1)}, s32[1,8,128]{2,1,0:T(8,128)}, u32[]{:S(2)}) copy-start(s32[1,8,128]{2,1,0:T(8,128)} %param.11) | copy-start | bytes 12292
  32.6 1.4 %copy-start.2 = (f32[1,362,1,8,128]{4,3,2,1,0:T(8,128)S(1)}, f32[1,362,1,8,128]{4,3,2,1,0:T(8,128)}, u32[]{:S(2)}) copy-start(f32[1,362,1,8,128]{4,3,2,1,0:T(8,128)} %get-tuple-element.30) | copy-start | bytes 4448260
  33.9 3.9 %copy-start.3 = (f32[362,1,8,128]{3,2,1,0:T(8,128)S(1)}, f32[362,1,8,128]{3,2,1,0:T(8,128)}, u32[]{:S(2)}) copy-start(f32[362,1,8,128]{3,2,1,0:T(8,128)} %param.15) | copy-start | bytes 4448260
  33.9 3.9 %copy-start.9 = (pred[128]{0:T(512)(128)(4,1)S(1)}, pred[128]{0:T(512)(128)(4,1)}, u32[]{:S(2)}) copy-start(pred[128]{0:T(512)(128)(4,1)} %constant.37.clone.1) | copy-start | bytes 388
  34.5 17.1 %collective-permute-start.3 = (f32[45,1,1,128]{3,0,2,1:T(8,128)S(1)}, f32[45,1,1,128]{3,0,2,1:T(8,128)S(1)}, u32[]{:S(2)}, u32[]{:S(2)}) collective-permute-start(f32[45,1,1,128]{3,0,2,1:T(8,128)S(1)} %convolution_bitcast_fusion.2), channel_id=1, source_target_pairs={{0,1},{1,2},{2,3},{3,4},{4,5},{5,6},{6,7},{8,9},{9,10},{10,11},{11... | collective-permute-start | bytes 69128 | tf_op jit(solution)/shard_map/ppermute | solution.py:17
  41.8 9.7 %collective-permute-start.2 = (f32[45,1,8,128]{3,0,2,1:T(8,128)S(1)}, f32[45,1,8,128]{3,0,2,1:T(8,128)S(1)}, u32[]{:S(2)}, u32[]{:S(2)}) collective-permute-start(f32[45,1,8,128]{3,0,2,1:T(8,128)S(1)} %copy.47), channel_id=1, source_target_pairs={{0,8},{8,16},{16,24},{24,32},{32,40},{40,48},{48,56},{56,64},{64,7... | collective-permute-start | bytes 552968 | tf_op jit(solution)/shard_map/ppermute | solution.py:17
  44.3 7.3 %copy-start.5 = (f32[45,1,8,128]{3,2,1,0:T(8,128)S(1)}, f32[45,1,8,128]{3,2,1,0:T(8,128)}, u32[]{:S(2)}) copy-start(f32[45,1,8,128]{3,2,1,0:T(8,128)} %param.8) | copy-start | bytes 552964
  44.4 7.3 %copy-start.6 = (f32[45,1,8,128]{3,2,1,0:T(8,128)S(1)}, f32[45,1,8,128]{3,2,1,0:T(8,128)}, u32[]{:S(2)}) copy-start(f32[45,1,8,128]{3,2,1,0:T(8,128)} %param.12) | copy-start | bytes 552964
  51.9 13.0 %collective-permute-start.4 = (f32[45,1,8,128]{3,0,2,1:T(8,128)S(1)}, f32[45,1,8,128]{3,0,2,1:T(8,128)S(1)}, u32[]{:S(2)}, u32[]{:S(2)}) collective-permute-start(f32[45,1,8,128]{3,0,2,1:T(8,128)S(1)} %get-tuple-element.21), channel_id=1, source_target_pairs={{8,0},{16,8},{24,16},{32,24},{40,32},{48,40},{56,48},{64,56},{72,6... | collective-permute-start | bytes 552968 | tf_op jit(solution)/shard_map/ppermute | solution.py:17
  53.8 10.6 %collective-permute-start.5 = (f32[45,1,1,128]{3,0,2,1:T(8,128)S(1)}, f32[45,1,1,128]{3,0,2,1:T(8,128)S(1)}, u32[]{:S(2)}, u32[]{:S(2)}) collective-permute-start(f32[45,1,1,128]{3,0,2,1:T(8,128)S(1)} %slice.95), channel_id=1, source_target_pairs={{1,0},{2,1},{3,2},{4,3},{5,4},{6,5},{7,6},{9,8},{10,9},{11,10},{12... | collective-permute-start | bytes 69128 | tf_op jit(solution)/shard_map/ppermute | solution.py:17
  63.3 1.1 %copy-start.1 = (f32[362,1,8,128]{3,0,2,1:T(8,128)}, f32[362,1,8,128]{3,0,2,1:T(8,128)S(1)}, u32[]{:S(2)}) copy-start(f32[362,1,8,128]{3,0,2,1:T(8,128)S(1)} %copy.53) | copy-start | bytes 4448260
  66.8 1.3 %slice-start = ((f32[362,1,8,128]{3,0,2,1:T(8,128)}), f32[362,1,7,128]{3,0,2,1:T(8,128)S(1)}, s32[]{:S(2)}) async-start(f32[362,1,8,128]{3,0,2,1:T(8,128)} %copy-done.1), calls=%async_computation | async-start | bytes 2637824 | tf_op jit(solution)/shard_map/slice | solution.py:71
  70.2 8.0 %copy-start.4 = (f32[362,1,8,128]{3,2,1,0:T(8,128)S(1)}, f32[362,1,8,128]{3,2,1,0:T(8,128)}, u32[]{:S(2)}) copy-start(f32[362,1,8,128]{3,2,1,0:T(8,128)} %param.15) | copy-start | bytes 4448260
  70.6 24.9 %collective-permute-start.7 = (f32[45,1,1,128]{3,0,2,1:T(8,128)S(1)}, f32[45,1,1,128]{3,0,2,1:T(8,128)S(1)}, u32[]{:S(2)}, u32[]{:S(2)}) collective-permute-start(f32[45,1,1,128]{3,0,2,1:T(8,128)S(1)} %convolution_bitcast_fusion.1), channel_id=1, source_target_pairs={{0,1},{1,2},{2,3},{3,4},{4,5},{5,6},{6,7},{8,9},{9,10},{10,11},{11... | collective-permute-start | bytes 69128 | tf_op jit(solution)/shard_map/ppermute | solution.py:17
  85.7 9.7 %collective-permute-start.6 = (f32[45,1,8,128]{3,0,2,1:T(8,128)S(1)}, f32[45,1,8,128]{3,0,2,1:T(8,128)S(1)}, u32[]{:S(2)}, u32[]{:S(2)}) collective-permute-start(f32[45,1,8,128]{3,0,2,1:T(8,128)S(1)} %copy.63), channel_id=1, source_target_pairs={{0,8},{8,16},{16,24},{24,32},{32,40},{40,48},{48,56},{56,64},{64,7... | collective-permute-start | bytes 552968 | tf_op jit(solution)/shard_map/ppermute | solution.py:17
where the time goes:
time: 97.6 us; the launch traced here: 97.1 us
  starting transfers between devices  36.8 us (38%)
  local copies, waits for them, and re-layouts  24.8 us (25%)
  matrix products  16.9 us (17%)
  waiting for transfers between devices  9.8 us (10%)
  other arithmetic  7.52 us (8%)
  between operations  1.29 us (1%)
    ppermute x8, starting transfers between devices, from_behind(): lax.ppermute(value, axis, [(source, source + steps) for source in range(l...  36.8 us
    unnamed x48, local copies, waits for them, and re-layouts  14.2 us
    dot_general x6, matrix products, to_sphere(): jnp.dot(basis, coef_rows.reshape(count, -1), precision=lax.Precision.HIGH...  11.9 us
    ppermute x8, waiting for transfers between devices, from_behind(): lax.ppermute(value, axis, [(source, source + steps) for source in range(l...  9.8 us
    dot_general x6, matrix products, to_harmonics(): jnp.dot(basis.T, amp_rows.reshape(count, -1), precision=lax.Precision.HIG...  5.05 us
    slice x1, local copies, waits for them, and re-layouts, per_device(): dual_grad[0] + STEP_DUAL * edge_diff(sphere_now, after_x, last_x, 1)  4.45 us
    sub x2, other arithmetic, per_device(): dual_sign - (inner_div(masked_x, 1) + inner_div(masked_y, 2) + backward_d...  3.02 us
    another operation x3, other arithmetic, per_device(): jnp.stack([stepped_x / shrink, stepped_y / shrink, stepped_z / shrink])  2.6 us
  transfers between devices with their start and end apart: 8, of which 2 were waited for; matrix products, arithmetic and copies ran while one was open for 33% of the time, Pallas kernels for 0%

commit v1 on v0

v1 whole, which is shorter than its diff:
```python
import jax
import jax.numpy as jnp
from jax import lax
from jax.experimental import pallas as pl
from jax.experimental.pallas import tpu as pltpu
from jax.sharding import PartitionSpec as P

STEP_PRIMAL = 0.25
STEP_DUAL = 0.02
TV_WEIGHT = 0.5

C, CP = 45, 48
N, NP = 362, 368
Y, Z = 8, 128
F32, BF16 = jnp.float32, jnp.bfloat16
MESH = pl.DeviceIdType.MESH
HBM = pl.BlockSpec(memory_space=pltpu.HBM)
VM = pl.BlockSpec(memory_space=pltpu.VMEM)


def halves(value):
    high = value.astype(BF16)
    return high, (value - high.astype(F32)).astype(BF16)


def main_kernel(sig, resp, bas, mask, coef, ext, dg, ds,
                dual, cout, eout,
                own, ex, ey, cur, sg, tgt, rdiv, rdx, rdy, up,
                mown, mx, my, bas_v, resp_v, fwd_w, bwd_w, q, r,
                ep_s, hx_s, hy_s, ep_r, hx_r, epy_r, hxd_r, hyd_r, hy_r, hx2_s, hy2_s, hx2_r, hy2_r,
                load_sem, dual_sem, a_s, a_r, b_s, b_r, f_s, f_r):
    gx, gy = lax.axis_index("gx"), lax.axis_index("gy")
    nx, ny = lax.axis_size("gx"), lax.axis_size("gy")
    xp, xm = lax.rem(gx + 1, nx), lax.rem(gx + nx - 1, nx)
    yp, ym = lax.rem(gy + 1, ny), lax.rem(gy + ny - 1, ny)
    keep_x = jnp.where(gx == nx - 1, 0.0, 1.0).astype(F32)
    keep_y = jnp.where(gy == ny - 1, 0.0, 1.0).astype(F32)

    barrier = pltpu.get_barrier_semaphore()
    for where in ((xm, gy), (xp, gy), (gx, ym), (gx, yp), (xm, yp), (xp, ym)):
        pl.semaphore_signal(barrier, inc=1, device_id=where, device_id_type=MESH)

    def rows_in(src, dst, base):
        return [pltpu.make_async_copy(src.at[:, y, :], dst.at[y, pl.ds(0, C), :], load_sem.at[base + y]) for y in range(Y)]
    ext_in = rows_in(ext, own, 0)
    cur_in = rows_in(coef, cur, 8)
    sig_in = rows_in(sig, sg, 16)
    bas_in = pltpu.make_async_copy(bas, bas_v, load_sem.at[24])
    resp_in = pltpu.make_async_copy(resp, resp_v, load_sem.at[25])
    mask_in = pltpu.make_async_copy(mask, mown, load_sem.at[26])
    dual_in = [[pltpu.make_async_copy((dg.at[a] if a < 3 else ds).at[:, y, :], dual.at[a, y, pl.ds(0, N), :], dual_sem.at[y, a])
                for a in range(4)] for y in range(Y)]
    for copy in ext_in + [mask_in, bas_in, resp_in]:
        copy.start()
    for copy in cur_in + sig_in:
        copy.start()
    for y in range(Y):
        for copy in dual_in[y]:
            copy.start()

    bas_in.wait()
    b_hi, b_lo = halves(bas_v[...])
    k_at = lax.broadcasted_iota(jnp.int32, (C, 256), 0)
    l_at = lax.broadcasted_iota(jnp.int32, (C, 256), 1)
    sel_hi = jnp.where((l_at == k_at) | (l_at == k_at + CP), 1.0, 0.0).astype(BF16)
    sel_lo = jnp.where(l_at == k_at + 2 * CP, 1.0, 0.0).astype(BF16)
    turn = (((0,), (0,)), ((), ()))
    fwd_w[...] = jnp.zeros((NP, 256), BF16)
    fwd_w[0:N, :] = (lax.dot_general(b_hi, sel_hi, turn, preferred_element_type=F32)
                     + lax.dot_general(b_lo, sel_lo, turn, preferred_element_type=F32)).astype(BF16)
    bwd_w[...] = jnp.zeros((2 * CP, 768), BF16)
    bwd_w[0:C, 0:N] = b_hi
    bwd_w[0:C, NP:NP + N] = b_hi
    bwd_w[CP:CP + C, 0:N] = b_lo
    q[:, 3 * CP:256, :] = jnp.zeros((2, 256 - 3 * CP, 4 * Z), BF16)
    r[:, 2 * NP:768, :] = jnp.zeros((2, 768 - 2 * NP, 2 * Z), BF16)
    for a in range(4):
        for y in range(Y):
            dual[a, y, pl.ds(N, NP - N), :] = jnp.zeros((NP - N, Z), F32)
    resp_in.wait()
    eye_f = lax.broadcasted_iota(jnp.int32, (CP, C), 0) == lax.broadcasted_iota(jnp.int32, (CP, C), 1)
    resp_c = jnp.sum(jnp.where(eye_f, jnp.broadcast_to(resp_v[...], (CP, C)), 0.0), axis=1, keepdims=True)

    mask_in.wait()
    for copy in ext_in:
        copy.wait()
    pl.semaphore_wait(barrier, 6)

    def send(src, dst, sems, at, where):
        copy = pltpu.make_async_remote_copy(src_ref=src, dst_ref=dst, send_sem=sems[0].at[at], recv_sem=sems[1].at[at],
                                            device_id=where, device_id_type=MESH)
        copy.start()
        return copy
    real = pl.ds(0, C)
    ab = (a_s, a_r)
    sent_a = {"ey": send(own.at[0, real, :], ey.at[real, :], ab, 8, (gx, ym))}
    for y in range(Y):
        sent_a[y] = send(own.at[y, real, :], ex.at[y, real, :], ab, y, (xm, gy))
    sent_a["my"] = send(mown, my, ab, 9, (gx, ym))
    sent_a["mx"] = send(mown, mx, ab, 10, (xm, gy))

    def recip(mask_row):
        m = jnp.broadcast_to(mask_row.astype(F32), (CP, Z))
        w = m * resp_c
        return 1.0 / (1.0 + STEP_PRIMAL * w * resp_c), w
    for y in range(Y):
        sig_in[y].wait()
        cur_in[y].wait()
        inv, w = recip(mown[y:y + 1, :])
        rdiv[y] = inv
        tgt[y] = STEP_PRIMAL * w * sg[y]

    pad_ok = lax.broadcasted_iota(jnp.int32, (CP, Z), 0) < C
    lane_last = lax.broadcasted_iota(jnp.int32, (1, Z), 1) == Z - 1
    z_keep = jnp.where(lane_last, 0.0, 1.0).astype(F32)

    def forward(y):
        slot = y % 2
        here = own[y]
        if y < Y - 1:
            dy = (own[y + 1] - here) * STEP_DUAL
        else:
            dy = (ey[...] - here) * (STEP_DUAL * keep_y)
        dx = (ex[y] - here) * (STEP_DUAL * keep_x)
        dz = (pltpu.roll(here, Z - 1, 1) - here) * (STEP_DUAL * z_keep)
        for a, field in enumerate((dx, dy, dz, here * STEP_DUAL)):
            hi, lo = halves(jnp.where(pad_ok, field, 0.0))
            at = slice(a * Z, (a + 1) * Z)
            q[slot, 0:CP, at] = hi
            q[slot, CP:2 * CP, at] = lo
            q[slot, 2 * CP:3 * CP, at] = hi
        mm = jnp.dot(fwd_w[...], q[slot], preferred_element_type=F32)
        sx = dual[0, y] + mm[:, 0:Z]
        sy = dual[1, y] + mm[:, Z:2 * Z]
        sz = dual[2, y] + mm[:, 2 * Z:3 * Z]
        scale = jnp.minimum(1.0, TV_WEIGHT * lax.rsqrt(sx * sx + sy * sy + sz * sz))
        dual[0, y] = sx * scale
        dual[1, y] = sy * scale
        dual[2, y] = sz * scale
        dual[3, y] = jnp.minimum(0.0, dual[3, y] + mm[:, 3 * Z:4 * Z])

    def project(slot, last_values):
        res = jnp.dot(bwd_w[...], r[slot], preferred_element_type=F32)
        return res[0:CP] + res[CP:2 * CP]

    def backward(y):
        slot = y % 2
        across = dual[1, y]
        if y == Y - 1:
            across = across * keep_y
        deep = dual[2, y] * z_keep
        w = dual[3, y] - across - deep + pltpu.roll(deep, 1, 1)
        if y > 0:
            w = w + dual[1, y - 1]
        for a, field in enumerate((w, dual[0, y])):
            hi, lo = halves(field)
            r[slot, 0:NP, a * Z:(a + 1) * Z] = hi
            r[slot, NP:2 * NP, a * Z:(a + 1) * Z] = lo
        res = project(slot, None)
        hx = res[:, Z:2 * Z] * keep_x
        harm = res[:, 0:Z] - hx
        return hx, (cur[y] - STEP_PRIMAL * harm + tgt[y]) * rdiv[y]

    def face_y():
        hi, lo = halves(dual[1, Y - 1])
        r[0, 0:NP, 0:Z] = hi
        r[0, NP:2 * NP, 0:Z] = lo
        return project(0, None)[:, 0:Z] * keep_y

    bb = (b_s, b_r)
    sent_b = {}
    for y in range(Y):
        if y == Y - 1:
            sent_a["ey"].wait_recv()
        sent_a[y].wait_recv()
        for copy in dual_in[y]:
            copy.wait()
        forward(y)
        if y == Y - 1:
            hy_s[...] = face_y()
            sent_b["hy"] = send(hy_s.at[real, :], hy_r.at[real, :], bb, 16, (gx, yp))
            sent_b["hyd"] = send(hy_s.at[real, :], hyd_r.at[real, :], bb, 17, (xm, yp))
        hx, u = backward(y)
        hx_s[y] = hx
        up[y] = u
        ep_s[y] = 2.0 * u - cur[y]
        if y == 0:
            sent_b["epy"] = send(ep_s.at[0, real, :], epy_r.at[real, :], bb, 18, (gx, ym))
            sent_b["hxd"] = send(hx_s.at[0, real, :], hxd_r.at[real, :], bb, 19, (xp, ym))
        sent_b["hx", y] = send(hx_s.at[y, real, :], hx_r.at[y, real, :], bb, y, (xp, gy))
        sent_b["ep", y] = send(ep_s.at[y, real, :], ep_r.at[y, real, :], bb, 8 + y, (xm, gy))

    sent_a["mx"].wait_recv()
    sent_a["my"].wait_recv()
    for y in range(Y):
        rdx[y] = recip(mx[y:y + 1, :])[0]
    rdy[...] = recip(my[0:1, :])[0]
    for key in sent_a:
        sent_a[key].wait_send()

    def finish(y):
        sent_b["hx", y].wait_recv()
        sent_b["ep", y].wait_recv()
        face = hx_r[y]
        above = hx_s[y]
        if y == 0:
            sent_b["hy"].wait_recv()
            sent_b["hyd"].wait_recv()
            face = face + hy_r[...]
            above = above + hyd_r[...]
        c_new = up[y] - STEP_PRIMAL * rdiv[y] * face
        own[y] = 2.0 * c_new - cur[y]
        cur[y] = c_new
        ex[y] = ep_r[y] - 2.0 * STEP_PRIMAL * rdx[y] * above

    ff = (f_s, f_r)
    sent_f = {}

    def second_back(y):
        hx, u = backward(y)
        hx2_s[y] = hx
        up[y] = u
        sent_f["hx", y] = send(hx2_s.at[y, real, :], hx2_r.at[y, real, :], ff, y, (xp, gy))

    finish(1)
    for y in range(1, Y):
        if y < Y - 1:
            finish(y + 1)
        else:
            sent_b["epy"].wait_recv()
            sent_b["hxd"].wait_recv()
            ey[...] = epy_r[...] - 2.0 * STEP_PRIMAL * rdy[...] * (hy_s[...] + hxd_r[...])
        forward(y)
        if y == Y - 1:
            hy2_s[...] = face_y()
            sent_f["hy"] = send(hy2_s.at[real, :], hy2_r.at[real, :], ff, 8, (gx, yp))
        if y > 1:
            second_back(y)
    finish(0)
    forward(0)
    second_back(0)
    second_back(1)
    for key in sent_b:
        sent_b[key].wait_send()

    for y in (2, 3, 4, 5, 6, 7, 0, 1):
        sent_f["hx", y].wait_recv()
        face = hx2_r[y]
        if y == 0:
            sent_f["hy"].wait_recv()
            face = face + hy2_r[...]
        c_new = up[y] - STEP_PRIMAL * rdiv[y] * face
        cout[y] = c_new
        eout[y] = 2.0 * c_new - cur[y]
    for key in sent_f:
        sent_f[key].wait_send()


def write_kernel(dual, cnew, enew, c_o, e_o, dg_o, ds_o, sem):
    copies = []
    for y in range(Y):
        for a in range(4):
            dst = dg_o.at[a] if a < 3 else ds_o
            copies.append((dual.at[a, y, pl.ds(0, N), :], dst.at[:, y, :]))
        copies.append((cnew.at[y, pl.ds(0, C), :], c_o.at[:, y, :]))
        copies.append((enew.at[y, pl.ds(0, C), :], e_o.at[:, y, :]))
    copies = [pltpu.make_async_copy(src, dst, sem.at[i]) for i, (src, dst) in enumerate(copies)]
    for copy in copies:
        copy.start()
    for copy in copies:
        copy.wait()


def per_device(signal, response, basis, mask, coefficients, extrapolated, dual_grad, dual_sign):
    block = pltpu.VMEM((Y, CP, Z), F32)
    face = pltpu.VMEM((CP, Z), F32)
    dma = pltpu.SemaphoreType.DMA
    dual, cnew, enew = pl.pallas_call(
        main_kernel,
        out_shape=(pltpu.VMEM((4, Y, NP, Z), F32), pltpu.VMEM((Y, CP, Z), F32), pltpu.VMEM((Y, CP, Z), F32)),
        in_specs=[HBM] * 8,
        out_specs=(VM, VM, VM),
        scratch_shapes=[
            block, block, face, block, block, block, block, block, face, block,
            pltpu.VMEM((Y, Z), jnp.int32), pltpu.VMEM((Y, Z), jnp.int32), pltpu.VMEM((Y, Z), jnp.int32),
            pltpu.VMEM((C, N), F32), pltpu.VMEM((1, C), F32),
            pltpu.VMEM((NP, 256), BF16), pltpu.VMEM((2 * CP, 768), BF16),
            pltpu.VMEM((2, 256, 4 * Z), BF16), pltpu.VMEM((2, 768, 2 * Z), BF16),
            block, block, face, block, block, face, face, face, face, block, face, block, face,
            dma((27,)), dma((Y, 4)), dma((11,)), dma((11,)), dma((20,)), dma((20,)), dma((9,)), dma((9,)),
        ],
        compiler_params=pltpu.CompilerParams(collective_id=0, has_side_effects=True, vmem_limit_bytes=40 * 2**20),
        name="steps",
    )(*(pltpu.with_memory_space_constraint(value, pltpu.HBM) for value in (
        signal.reshape(C, Y, Z), response.reshape(1, C), basis.T, mask.reshape(Y, Z), coefficients.reshape(C, Y, Z),
        extrapolated.reshape(C, Y, Z), dual_grad.reshape(3, N, Y, Z), dual_sign.reshape(N, Y, Z),
    )))
    c_o, e_o, dg_o, ds_o = pl.pallas_call(
        write_kernel,
        out_shape=(jax.ShapeDtypeStruct((C, Y, Z), F32), jax.ShapeDtypeStruct((C, Y, Z), F32),
                   jax.ShapeDtypeStruct((3, N, Y, Z), F32), jax.ShapeDtypeStruct((N, Y, Z), F32)),
        in_specs=[VM] * 3,
        out_specs=(HBM,) * 4,
        scratch_shapes=[dma((6 * Y,))],
        compiler_params=pltpu.CompilerParams(vmem_limit_bytes=16 * 2**20),
        name="write",
    )(*(pltpu.with_memory_space_constraint(value, pltpu.VMEM) for value in (dual, cnew, enew)))
    return (c_o.reshape(coefficients.shape), e_o.reshape(coefficients.shape),
            dg_o.reshape(dual_grad.shape), ds_o.reshape(dual_sign.shape))


def solution(mesh):
    in_specs = (
        P(None, "gx", "gy", None), P(), P(), P("gx", "gy", None), P(None, "gx", "gy", None),
        P(None, "gx", "gy", None), P(None, None, "gx", "gy", None), P(None, "gx", "gy", None),
    )
    out_specs = (
        P(None, "gx", "gy", None), P(None, "gx", "gy", None), P(None, None, "gx", "gy", None), P(None, "gx", "gy", None),
    )
    return jax.shard_map(per_device, mesh=mesh, in_specs=in_specs, out_specs=out_specs, check_vma=False)
```

time: 97.6 us -> 35.2 us (0.36)
  the two profiles are of different devices: /device:TPU:26 before, /device:TPU:2 now
where the time goes in v1:
time: 35.2 us; the launch traced here: 35.1 us
  Pallas kernels  34.4 us (98%)
  between operations  0.64 us (2%)
    pallas_call x1, Pallas kernels, per_device(): pl.pallas_call(main_kernel, out_shape=(pltpu.VMEM((4, Y, NP, Z), F32), pl...  31.4 us
    pallas_call x1, Pallas kernels, per_device(): pl.pallas_call(write_kernel, out_shape=(jax.ShapeDtypeStruct((C, Y, Z), F...  3.04 us

profile of v1, /device:TPU:2, one launch (start us, length us, event | category | flops | bytes accessed | tf_op | source)
XLA Modules:
  0.0 35.1 jit_solution(6328541463320201399)
XLA Ops:
  0.6 31.4 %steps.1 = (f32[4,8,368,128]{3,2,1,0:T(8,128)S(1)}, f32[8,48,128]{2,1,0:T(8,128)S(1)}, f32[8,48,128]{2,1,0:T(8,128)S(1)}) custom-call(f32[45,8,128]{2,1,0:T(8,128)} %bitcast.22, f32[1,45]{1,0:T(1,128)} %bitcast.27, f32[45,362]{1,0:T(8,128)} %bitcast.25, s32[8,128]{1,0:T(8,128)} %bitcast.26, f32[45,8,128]{2,1,0:T(8,128)} %bitcast.23, f32[45,8,128]{2,1,0:T(8,128)} %bitcast.24, ...), custom_call_target="tpu_custom_call" | custom-call | tf_op jit(solution)/shard_map/steps/pallas_call | solution.py:278
  32.0 3.0 %write.1 = (f32[45,8,128]{2,1,0:T(8,128)}, f32[45,8,128]{2,1,0:T(8,128)}, f32[3,362,8,128]{3,2,1,0:T(8,128)}, f32[362,8,128]{2,1,0:T(8,128)}) custom-call(f32[4,8,368,128]{3,2,1,0:T(8,128)S(1)} %get-tuple-element.11.dual, f32[8,48,128]{2,1,0:T(8,128)S(1)} %get-tuple-element.12.cnew, f32[8,48,128]{2,1,0:T(8,128)S(1)} %get-tuple-element.13.enew), custom_call_target="tpu_custom_call" | custom-call | tf_op jit(solution)/shard_map/write/pallas_call | solution.py:298

commit v2 on v1

--- a/solution.py
+++ b/solution.py
@@ -31,14 +31,22 @@
                 load_sem, dual_sem, a_s, a_r, b_s, b_r, f_s, f_r):
     gx, gy = lax.axis_index("gx"), lax.axis_index("gy")
     nx, ny = lax.axis_size("gx"), lax.axis_size("gy")
-    xp, xm = lax.rem(gx + 1, nx), lax.rem(gx + nx - 1, nx)
-    yp, ym = lax.rem(gy + 1, ny), lax.rem(gy + ny - 1, ny)
-    keep_x = jnp.where(gx == nx - 1, 0.0, 1.0).astype(F32)
-    keep_y = jnp.where(gy == ny - 1, 0.0, 1.0).astype(F32)
+    has_xp, has_xm, has_yp, has_ym = gx < nx - 1, gx > 0, gy < ny - 1, gy > 0
+    to_xp, to_xm, to_yp, to_ym = (gx + 1, gy), (gx - 1, gy), (gx, gy + 1), (gx, gy - 1)
+    up_left, down_right = (gx - 1, gy + 1), (gx + 1, gy - 1)
+    has_ul, has_dr = jnp.logical_and(has_xm, has_yp), jnp.logical_and(has_xp, has_ym)
+    keep_x = jnp.where(has_xp, 1.0, 0.0).astype(F32)
+    keep_y = jnp.where(has_yp, 1.0, 0.0).astype(F32)
 
     barrier = pltpu.get_barrier_semaphore()
-    for where in ((xm, gy), (xp, gy), (gx, ym), (gx, yp), (xm, yp), (xp, ym)):
-        pl.semaphore_signal(barrier, inc=1, device_id=where, device_id_type=MESH)
+
+    @pl.when(has_xp)
+    def _():
+        pl.semaphore_signal(barrier, inc=1, device_id=to_xp, device_id_type=MESH)
+
+    @pl.when(has_yp)
+    def _():
+        pl.semaphore_signal(barrier, inc=1, device_id=to_yp, device_id_type=MESH)
 
     def rows_in(src, dst, base):
         return [pltpu.make_async_copy(src.at[:, y, :], dst.at[y, pl.ds(0, C), :], load_sem.at[base + y]) for y in range(Y)]
@@ -57,6 +65,38 @@
     for y in range(Y):
         for copy in dual_in[y]:
             copy.start()
+
+    zeros, face0 = jnp.zeros((Y, CP, Z), F32), jnp.zeros((CP, Z), F32)
+
+    @pl.when(jnp.logical_not(has_xp))
+    def _():
+        ex[...] = zeros
+        ep_r[...] = zeros
+        mx[...] = jnp.zeros((Y, Z), jnp.int32)
+
+    @pl.when(jnp.logical_not(has_xm))
+    def _():
+        hx_r[...] = zeros
+        hx2_r[...] = zeros
+
+    @pl.when(jnp.logical_not(has_yp))
+    def _():
+        ey[...] = face0
+        epy_r[...] = face0
+        my[...] = jnp.zeros((Y, Z), jnp.int32)
+
+    @pl.when(jnp.logical_not(has_ym))
+    def _():
+        hy_r[...] = face0
+        hy2_r[...] = face0
+
+    @pl.when(jnp.logical_not(has_ul))
+    def _():
+        hxd_r[...] = face0
+
+    @pl.when(jnp.logical_not(has_dr))
+    def _():
+        hyd_r[...] = face0
 
     bas_in.wait()
     b_hi, b_lo = halves(bas_v[...])
@@ -84,28 +124,40 @@
     mask_in.wait()
     for copy in ext_in:
         copy.wait()
-    pl.semaphore_wait(barrier, 6)
-
-    def send(src, dst, sems, at, where):
-        copy = pltpu.make_async_remote_copy(src_ref=src, dst_ref=dst, send_sem=sems[0].at[at], recv_sem=sems[1].at[at],
-                                            device_id=where, device_id_type=MESH)
-        copy.start()
-        return copy
+
+    @pl.when(jnp.logical_or(has_xm, has_ym))
+    def _():
+        pl.semaphore_wait(barrier, jnp.minimum(gx, 1) + jnp.minimum(gy, 1))
+
+    class Message:
+        def __init__(self, src, dst, sems, at, where, goes, comes):
+            self.goes, self.comes = goes, comes
+            self.copy = pltpu.make_async_remote_copy(src_ref=src, dst_ref=dst, send_sem=sems[0].at[at], recv_sem=sems[1].at[at],
+                                                     device_id=where, device_id_type=MESH)
+            pl.when(goes)(self.copy.start)
+
+        def arrived(self):
+            pl.when(self.comes)(self.copy.wait_recv)
+
+        def left(self):
+            pl.when(self.goes)(self.copy.wait_send)
+
     real = pl.ds(0, C)
     ab = (a_s, a_r)
-    sent_a = {"ey": send(own.at[0, real, :], ey.at[real, :], ab, 8, (gx, ym))}
-    for y in range(Y):
-        sent_a[y] = send(own.at[y, real, :], ex.at[y, real, :], ab, y, (xm, gy))
-    sent_a["my"] = send(mown, my, ab, 9, (gx, ym))
-    sent_a["mx"] = send(mown, mx, ab, 10, (xm, gy))
+    sent_a = {"ey": Message(own.at[0, real, :], ey.at[real, :], ab, 4, to_ym, has_ym, has_yp)}
+    for p in range(4):
+        two = pl.ds(2 * p, 2)
+        sent_a[p] = Message(own.at[two, real, :], ex.at[two, real, :], ab, p, to_xm, has_xm, has_xp)
+    sent_a["my"] = Message(mown, my, ab, 5, to_ym, has_ym, has_yp)
+    sent_a["mx"] = Message(mown, mx, ab, 6, to_xm, has_xm, has_xp)
 
     def recip(mask_row):
         m = jnp.broadcast_to(mask_row.astype(F32), (CP, Z))
         w = m * resp_c
         return 1.0 / (1.0 + STEP_PRIMAL * w * resp_c), w
-    for y in range(Y):
-        sig_in[y].wait()
-        cur_in[y].wait()
+    for copy in sig_in + cur_in:
+        copy.wait()
+    for y in range(Y):
         inv, w = recip(mown[y:y + 1, :])
         rdiv[y] = inv
         tgt[y] = STEP_PRIMAL * w * sg[y]
@@ -114,37 +166,46 @@
     lane_last = lax.broadcasted_iota(jnp.int32, (1, Z), 1) == Z - 1
     z_keep = jnp.where(lane_last, 0.0, 1.0).astype(F32)
 
-    def forward(y):
-        slot = y % 2
-        here = own[y]
-        if y < Y - 1:
-            dy = (own[y + 1] - here) * STEP_DUAL
-        else:
-            dy = (ey[...] - here) * (STEP_DUAL * keep_y)
-        dx = (ex[y] - here) * (STEP_DUAL * keep_x)
-        dz = (pltpu.roll(here, Z - 1, 1) - here) * (STEP_DUAL * z_keep)
-        for a, field in enumerate((dx, dy, dz, here * STEP_DUAL)):
+    def lift(slot, fields):
+        for a, field in enumerate(fields):
             hi, lo = halves(jnp.where(pad_ok, field, 0.0))
             at = slice(a * Z, (a + 1) * Z)
             q[slot, 0:CP, at] = hi
             q[slot, CP:2 * CP, at] = lo
             q[slot, 2 * CP:3 * CP, at] = hi
-        mm = jnp.dot(fwd_w[...], q[slot], preferred_element_type=F32)
-        sx = dual[0, y] + mm[:, 0:Z]
-        sy = dual[1, y] + mm[:, Z:2 * Z]
-        sz = dual[2, y] + mm[:, 2 * Z:3 * Z]
+        mm = jnp.dot(fwd_w[...], q[slot, :, 0:len(fields) * Z], preferred_element_type=F32)
+        return [mm[:, a * Z:(a + 1) * Z] for a in range(len(fields))]
+
+    def diff_x(y):
+        return (ex[y] - own[y]) * (STEP_DUAL * keep_x)
+
+    def diff_y(y):
+        if y < Y - 1:
+            return (own[y + 1] - own[y]) * STEP_DUAL
+        return (ey[...] - own[y]) * (STEP_DUAL * keep_y)
+
+    def diff_z(y):
+        return (pltpu.roll(own[y], Z - 1, 1) - own[y]) * (STEP_DUAL * z_keep)
+
+    def shrink(y, sx, sy, sz):
         scale = jnp.minimum(1.0, TV_WEIGHT * lax.rsqrt(sx * sx + sy * sy + sz * sz))
         dual[0, y] = sx * scale
         dual[1, y] = sy * scale
         dual[2, y] = sz * scale
-        dual[3, y] = jnp.minimum(0.0, dual[3, y] + mm[:, 3 * Z:4 * Z])
-
-    def project(slot, last_values):
-        res = jnp.dot(bwd_w[...], r[slot], preferred_element_type=F32)
-        return res[0:CP] + res[CP:2 * CP]
-
-    def backward(y):
-        slot = y % 2
+
+    def sign(y, amp):
+        dual[3, y] = jnp.minimum(0.0, dual[3, y] + amp)
+
+    def drop(slot, values):
+        for a, value in enumerate(values):
+            hi, lo = halves(value)
+            r[slot, 0:NP, a * Z:(a + 1) * Z] = hi
+            r[slot, NP:2 * NP, a * Z:(a + 1) * Z] = lo
+        res = jnp.dot(bwd_w[...], r[slot, :, 0:len(values) * Z], preferred_element_type=F32)
+        res = res[0:CP] + res[CP:2 * CP]
+        return [res[:, a * Z:(a + 1) * Z] for a in range(len(values))]
+
+    def inner(y):
         across = dual[1, y]
         if y == Y - 1:
             across = across * keep_y
@@ -152,60 +213,72 @@
         w = dual[3, y] - across - deep + pltpu.roll(deep, 1, 1)
         if y > 0:
             w = w + dual[1, y - 1]
-        for a, field in enumerate((w, dual[0, y])):
-            hi, lo = halves(field)
-            r[slot, 0:NP, a * Z:(a + 1) * Z] = hi
-            r[slot, NP:2 * NP, a * Z:(a + 1) * Z] = lo
-        res = project(slot, None)
-        hx = res[:, Z:2 * Z] * keep_x
-        harm = res[:, 0:Z] - hx
-        return hx, (cur[y] - STEP_PRIMAL * harm + tgt[y]) * rdiv[y]
-
-    def face_y():
-        hi, lo = halves(dual[1, Y - 1])
-        r[0, 0:NP, 0:Z] = hi
-        r[0, NP:2 * NP, 0:Z] = lo
-        return project(0, None)[:, 0:Z] * keep_y
+        return w
+
+    def advance(y, harm):
+        return (cur[y] - STEP_PRIMAL * harm + tgt[y]) * rdiv[y]
+
+    for y in range(Y):
+        for copy in dual_in[y]:
+            copy.wait()
+    for y in range(Y):
+        fields = [diff_z(y), own[y] * STEP_DUAL]
+        if y < Y - 1:
+            fields.append(diff_y(y))
+        mm = lift(y % 2, fields)
+        dual[2, y] = dual[2, y] + mm[0]
+        sign(y, mm[1])
+        if y < Y - 1:
+            dual[1, y] = dual[1, y] + mm[2]
 
     bb = (b_s, b_r)
     sent_b = {}
-    for y in range(Y):
-        if y == Y - 1:
-            sent_a["ey"].wait_recv()
-        sent_a[y].wait_recv()
-        for copy in dual_in[y]:
-            copy.wait()
-        forward(y)
-        if y == Y - 1:
-            hy_s[...] = face_y()
-            sent_b["hy"] = send(hy_s.at[real, :], hy_r.at[real, :], bb, 16, (gx, yp))
-            sent_b["hyd"] = send(hy_s.at[real, :], hyd_r.at[real, :], bb, 17, (xm, yp))
-        hx, u = backward(y)
-        hx_s[y] = hx
-        up[y] = u
-        ep_s[y] = 2.0 * u - cur[y]
-        if y == 0:
-            sent_b["epy"] = send(ep_s.at[0, real, :], epy_r.at[real, :], bb, 18, (gx, ym))
-            sent_b["hxd"] = send(hx_s.at[0, real, :], hxd_r.at[real, :], bb, 19, (xp, ym))
-        sent_b["hx", y] = send(hx_s.at[y, real, :], hx_r.at[y, real, :], bb, y, (xp, gy))
-        sent_b["ep", y] = send(ep_s.at[y, real, :], ep_r.at[y, real, :], bb, 8 + y, (xm, gy))
-
-    sent_a["mx"].wait_recv()
-    sent_a["my"].wait_recv()
+    for p in range(4):
+        ya, yb = 2 * p, 2 * p + 1
+        two = pl.ds(ya, 2)
+        sent_a[p].arrived()
+        if yb == Y - 1:
+            sent_a["ey"].arrived()
+            mm = lift(p % 2, [diff_x(yb), diff_y(yb), diff_x(ya)])
+            shrink(yb, dual[0, yb] + mm[0], dual[1, yb] + mm[1], dual[2, yb])
+            hy_s[...] = drop(0, [dual[1, yb]])[0] * keep_y
+            sent_b["hy"] = Message(hy_s.at[real, :], hy_r.at[real, :], bb, 8, to_yp, has_yp, has_ym)
+            sent_b["hyd"] = Message(hy_s.at[real, :], hyd_r.at[real, :], bb, 9, up_left, has_ul, has_dr)
+            shrink(ya, dual[0, ya] + mm[2], dual[1, ya], dual[2, ya])
+        else:
+            mm = lift(p % 2, [diff_x(ya), diff_x(yb)])
+            for y, part in ((ya, mm[0]), (yb, mm[1])):
+                shrink(y, dual[0, y] + part, dual[1, y], dual[2, y])
+        faces = drop(0, [dual[0, ya], dual[0, yb]])
+        harms = drop(1, [inner(ya), inner(yb)])
+        for y, face, harm in ((ya, faces[0], harms[0]), (yb, faces[1], harms[1])):
+            face = face * keep_x
+            hx_s[y] = face
+            u = advance(y, harm - face)
+            up[y] = u
+            ep_s[y] = 2.0 * u - cur[y]
+        if p == 0:
+            sent_b["epy"] = Message(ep_s.at[0, real, :], epy_r.at[real, :], bb, 10, to_ym, has_ym, has_yp)
+            sent_b["hxd"] = Message(hx_s.at[0, real, :], hxd_r.at[real, :], bb, 11, down_right, has_dr, has_ul)
+        sent_b["hx", p] = Message(hx_s.at[two, real, :], hx_r.at[two, real, :], bb, p, to_xp, has_xp, has_xm)
+        sent_b["ep", p] = Message(ep_s.at[two, real, :], ep_r.at[two, real, :], bb, 4 + p, to_xm, has_xm, has_xp)
+
+    sent_a["mx"].arrived()
+    sent_a["my"].arrived()
     for y in range(Y):
         rdx[y] = recip(mx[y:y + 1, :])[0]
     rdy[...] = recip(my[0:1, :])[0]
     for key in sent_a:
-        sent_a[key].wait_send()
+        sent_a[key].left()
+
+    def pair_here(p):
+        sent_b["hx", p].arrived()
+        sent_b["ep", p].arrived()
 
     def finish(y):
-        sent_b["hx", y].wait_recv()
-        sent_b["ep", y].wait_recv()
         face = hx_r[y]
         above = hx_s[y]
         if y == 0:
-            sent_b["hy"].wait_recv()
-            sent_b["hyd"].wait_recv()
             face = face + hy_r[...]
             above = above + hyd_r[...]
         c_new = up[y] - STEP_PRIMAL * rdiv[y] * face
@@ -216,44 +289,68 @@
     ff = (f_s, f_r)
     sent_f = {}
 
-    def second_back(y):
-        hx, u = backward(y)
-        hx2_s[y] = hx
-        up[y] = u
-        sent_f["hx", y] = send(hx2_s.at[y, real, :], hx2_r.at[y, real, :], ff, y, (xp, gy))
-
-    finish(1)
-    for y in range(1, Y):
-        if y < Y - 1:
-            finish(y + 1)
-        else:
-            sent_b["epy"].wait_recv()
-            sent_b["hxd"].wait_recv()
-            ey[...] = epy_r[...] - 2.0 * STEP_PRIMAL * rdy[...] * (hy_s[...] + hxd_r[...])
-        forward(y)
-        if y == Y - 1:
-            hy2_s[...] = face_y()
-            sent_f["hy"] = send(hy2_s.at[real, :], hy2_r.at[real, :], ff, 8, (gx, yp))
-        if y > 1:
-            second_back(y)
+    def forward(y):
+        mm = lift(y % 2, [diff_x(y), diff_y(y), diff_z(y), own[y] * STEP_DUAL])
+        shrink(y, dual[0, y] + mm[0], dual[1, y] + mm[1], dual[2, y] + mm[2])
+        sign(y, mm[3])
+
+    def send_faces(rows):
+        for y, face in zip(rows, drop(0, [dual[0, y] for y in rows])):
+            hx2_s[y] = face * keep_x
+        for y in rows:
+            sent_f["hx", y] = Message(hx2_s.at[y, real, :], hx2_r.at[y, real, :], ff, y, to_xp, has_xp, has_xm)
+
+    pair_here(0)
+    pair_here(1)
+    for y in (1, 2, 3):
+        finish(y)
+    forward(1)
+    forward(2)
+    send_faces((1, 2))
+    pair_here(2)
+    finish(4)
+    finish(5)
+    forward(3)
+    forward(4)
+    send_faces((3, 4))
+    pair_here(3)
+    sent_b["epy"].arrived()
+    sent_b["hxd"].arrived()
+    finish(6)
+    finish(7)
+    ey[...] = epy_r[...] - 2.0 * STEP_PRIMAL * rdy[...] * (hy_s[...] + hxd_r[...])
+    forward(7)
+    hy2_s[...] = drop(0, [dual[1, Y - 1]])[0] * keep_y
+    sent_f["hy"] = Message(hy2_s.at[real, :], hy2_r.at[real, :], ff, 8, to_yp, has_yp, has_ym)
+    forward(5)
+    forward(6)
+    send_faces((6, 7))
+    send_faces((5,))
+    sent_b["hy"].arrived()
+    sent_b["hyd"].arrived()
     finish(0)
     forward(0)
-    second_back(0)
-    second_back(1)
+    send_faces((0,))
+
+    for p in range(4):
+        ya, yb = 2 * p, 2 * p + 1
+        harms = drop(p % 2, [inner(ya), inner(yb)])
+        for y, harm in ((ya, harms[0]), (yb, harms[1])):
+            up[y] = advance(y, harm - hx2_s[y])
     for key in sent_b:
-        sent_b[key].wait_send()
-
-    for y in (2, 3, 4, 5, 6, 7, 0, 1):
-        sent_f["hx", y].wait_recv()
+        sent_b[key].left()
+
+    for y in (1, 2, 3, 4, 6, 7, 5, 0):
+        sent_f["hx", y].arrived()
         face = hx2_r[y]
         if y == 0:
-            sent_f["hy"].wait_recv()
+            sent_f["hy"].arrived()
             face = face + hy2_r[...]
         c_new = up[y] - STEP_PRIMAL * rdiv[y] * face
         cout[y] = c_new
         eout[y] = 2.0 * c_new - cur[y]
     for key in sent_f:
-        sent_f[key].wait_send()
+        sent_f[key].left()
 
 
 def write_kernel(dual, cnew, enew, c_o, e_o, dg_o, ds_o, sem):
@@ -287,7 +384,7 @@
             pltpu.VMEM((NP, 256), BF16), pltpu.VMEM((2 * CP, 768), BF16),
             pltpu.VMEM((2, 256, 4 * Z), BF16), pltpu.VMEM((2, 768, 2 * Z), BF16),
             block, block, face, block, block, face, face, face, face, block, face, block, face,
-            dma((27,)), dma((Y, 4)), dma((11,)), dma((11,)), dma((20,)), dma((20,)), dma((9,)), dma((9,)),
+            dma((27,)), dma((Y, 4)), dma((7,)), dma((7,)), dma((12,)), dma((12,)), dma((9,)), dma((9,)),
         ],
         compiler_params=pltpu.CompilerParams(collective_id=0, has_side_effects=True, vmem_limit_bytes=40 * 2**20),
         name="steps",

time: 35.2 us -> 31.1 us (0.88)
  the two profiles are of different devices: /device:TPU:2 before, /device:TPU:26 now
where the time goes in v2:
time: 31.1 us; the launch traced here: 30.8 us
  Pallas kernels  30.2 us (97%)
  between operations  0.64 us (2%)
    pallas_call x1, Pallas kernels, per_device(): pl.pallas_call(main_kernel, out_shape=(pltpu.VMEM((4, Y, NP, Z), F32), pl...  27.1 us
    pallas_call x1, Pallas kernels, per_device(): pl.pallas_call(write_kernel, out_shape=(jax.ShapeDtypeStruct((C, Y, Z), F...  3.04 us

profile of v2, /device:TPU:26, one launch (start us, length us, event | category | flops | bytes accessed | tf_op | source)
XLA Modules:
  0.0 30.8 jit_solution(14519106471134428532)
XLA Ops:
  0.6 27.1 %steps.1 = (f32[4,8,368,128]{3,2,1,0:T(8,128)S(1)}, f32[8,48,128]{2,1,0:T(8,128)S(1)}, f32[8,48,128]{2,1,0:T(8,128)S(1)}) custom-call(f32[45,8,128]{2,1,0:T(8,128)} %bitcast.22, f32[1,45]{1,0:T(1,128)} %bitcast.27, f32[45,362]{1,0:T(8,128)} %bitcast.25, s32[8,128]{1,0:T(8,128)} %bitcast.26, f32[45,8,128]{2,1,0:T(8,128)} %bitcast.23, f32[45,8,128]{2,1,0:T(8,128)} %bitcast.24, ...), custom_call_target="tpu_custom_call" | custom-call | tf_op jit(solution)/shard_map/steps/pallas_call | solution.py:375
  27.8 3.0 %write.1 = (f32[45,8,128]{2,1,0:T(8,128)}, f32[45,8,128]{2,1,0:T(8,128)}, f32[3,362,8,128]{3,2,1,0:T(8,128)}, f32[362,8,128]{2,1,0:T(8,128)}) custom-call(f32[4,8,368,128]{3,2,1,0:T(8,128)S(1)} %get-tuple-element.11.dual, f32[8,48,128]{2,1,0:T(8,128)S(1)} %get-tuple-element.12.cnew, f32[8,48,128]{2,1,0:T(8,128)S(1)} %get-tuple-element.13.enew), custom_call_target="tpu_custom_call" | custom-call | tf_op jit(solution)/shard_map/write/pallas_call | solution.py:395

commit v3 on v2

--- a/solution.py
+++ b/solution.py
@@ -28,25 +28,39 @@
                 own, ex, ey, cur, sg, tgt, rdiv, rdx, rdy, up,
                 mown, mx, my, bas_v, resp_v, fwd_w, bwd_w, q, r,
                 ep_s, hx_s, hy_s, ep_r, hx_r, epy_r, hxd_r, hyd_r, hy_r, hx2_s, hy2_s, hx2_r, hy2_r,
-                load_sem, dual_sem, a_s, a_r, b_s, b_r, f_s, f_r):
+                load_sem, dual_sem, a_s, a_r, b_s, b_r, f_s, f_r, ready, ready_d):
     gx, gy = lax.axis_index("gx"), lax.axis_index("gy")
     nx, ny = lax.axis_size("gx"), lax.axis_size("gy")
     has_xp, has_xm, has_yp, has_ym = gx < nx - 1, gx > 0, gy < ny - 1, gy > 0
     to_xp, to_xm, to_yp, to_ym = (gx + 1, gy), (gx - 1, gy), (gx, gy + 1), (gx, gy - 1)
     up_left, down_right = (gx - 1, gy + 1), (gx + 1, gy - 1)
     has_ul, has_dr = jnp.logical_and(has_xm, has_yp), jnp.logical_and(has_xp, has_ym)
+    far_above = jnp.logical_and(lax.rem(gx, 8) == 7, has_xp)
+    far_below = jnp.logical_and(lax.rem(gx, 8) == 0, has_xm)
     keep_x = jnp.where(has_xp, 1.0, 0.0).astype(F32)
     keep_y = jnp.where(has_yp, 1.0, 0.0).astype(F32)
 
+    odd = lax.rem(gy, 2) == 1
+    even = jnp.logical_not(odd)
+    head = lax.rem(gx, 8) == 0
+    tail = jnp.logical_or(lax.rem(gx, 8) == 7, gx == nx - 1)
     barrier = pltpu.get_barrier_semaphore()
 
-    @pl.when(has_xp)
-    def _():
-        pl.semaphore_signal(barrier, inc=1, device_id=to_xp, device_id_type=MESH)
-
-    @pl.when(has_yp)
-    def _():
-        pl.semaphore_signal(barrier, inc=1, device_id=to_yp, device_id_type=MESH)
+    def both(*flags):
+        out = flags[0]
+        for flag in flags[1:]:
+            out = jnp.logical_and(out, flag)
+        return out
+
+    def greet(sem, when, where):
+        @pl.when(when)
+        def _():
+            pl.semaphore_signal(sem, inc=1, device_id=where, device_id_type=MESH)
+
+    greet(barrier, has_xp, to_xp)
+    greet(barrier, both(even, has_yp), to_yp)
+    greet(barrier, both(even, has_ym), to_ym)
+    greet(barrier, both(even, has_dr), down_right)
 
     def rows_in(src, dst, base):
         return [pltpu.make_async_copy(src.at[:, y, :], dst.at[y, pl.ds(0, C), :], load_sem.at[base + y]) for y in range(Y)]
@@ -65,6 +79,49 @@
     for y in range(Y):
         for copy in dual_in[y]:
             copy.start()
+
+    left, up_there = jnp.minimum(gx, 1), jnp.minimum(ny - 1 - gy, 1)
+
+    @pl.when(jnp.logical_or(has_xm, odd))
+    def _():
+        pl.semaphore_wait(barrier, left + lax.rem(gy, 2) * (1 + up_there + left * up_there))
+
+    greet(ready, both(odd, has_ul, jnp.logical_not(head)), up_left)
+    greet(ready, both(odd, has_yp, tail), to_yp)
+    greet(ready_d, both(odd, has_ul, head), up_left)
+
+    for copy in ext_in:
+        copy.wait()
+
+    class Message:
+        def __init__(self, src, dst, sems, at, where, goes, comes, now=True):
+            self.goes, self.comes = goes, comes
+            self.copy = pltpu.make_async_remote_copy(src_ref=src, dst_ref=dst, send_sem=sems[0].at[at], recv_sem=sems[1].at[at],
+                                                     device_id=where, device_id_type=MESH)
+            if now:
+                self.go()
+
+        def go(self):
+            pl.when(self.goes)(self.copy.start)
+
+        def arrived(self):
+            pl.when(self.comes)(self.copy.wait_recv)
+
+        def left(self):
+            pl.when(self.goes)(self.copy.wait_send)
+
+    real = pl.ds(0, C)
+    ab = (a_s, a_r)
+    sent_a = {}
+    face_copy = pltpu.make_async_remote_copy(src_ref=own.at[0, real, :], dst_ref=ey.at[real, :], send_sem=a_s.at[4], recv_sem=a_r.at[4],
+                                             device_id=to_ym, device_id_type=MESH)
+
+    @pl.when(both(odd, has_ym))
+    def _():
+        face_copy.start()
+    for p in (3, 0, 1, 2):
+        two = pl.ds(2 * p, 2)
+        sent_a[p] = Message(own.at[two, real, :], ex.at[two, real, :], ab, p, to_xm, has_xm, has_xp)
 
     zeros, face0 = jnp.zeros((Y, CP, Z), F32), jnp.zeros((CP, Z), F32)
 
@@ -122,34 +179,6 @@
     resp_c = jnp.sum(jnp.where(eye_f, jnp.broadcast_to(resp_v[...], (CP, C)), 0.0), axis=1, keepdims=True)
 
     mask_in.wait()
-    for copy in ext_in:
-        copy.wait()
-
-    @pl.when(jnp.logical_or(has_xm, has_ym))
-    def _():
-        pl.semaphore_wait(barrier, jnp.minimum(gx, 1) + jnp.minimum(gy, 1))
-
-    class Message:
-        def __init__(self, src, dst, sems, at, where, goes, comes):
-            self.goes, self.comes = goes, comes
-            self.copy = pltpu.make_async_remote_copy(src_ref=src, dst_ref=dst, send_sem=sems[0].at[at], recv_sem=sems[1].at[at],
-                                                     device_id=where, device_id_type=MESH)
-            pl.when(goes)(self.copy.start)
-
-        def arrived(self):
-            pl.when(self.comes)(self.copy.wait_recv)
-
-        def left(self):
-            pl.when(self.goes)(self.copy.wait_send)
-
-    real = pl.ds(0, C)
-    ab = (a_s, a_r)
-    sent_a = {"ey": Message(own.at[0, real, :], ey.at[real, :], ab, 4, to_ym, has_ym, has_yp)}
-    for p in range(4):
-        two = pl.ds(2 * p, 2)
-        sent_a[p] = Message(own.at[two, real, :], ex.at[two, real, :], ab, p, to_xm, has_xm, has_xp)
-    sent_a["my"] = Message(mown, my, ab, 5, to_ym, has_ym, has_yp)
-    sent_a["mx"] = Message(mown, mx, ab, 6, to_xm, has_xm, has_xp)
 
     def recip(mask_row):
         m = jnp.broadcast_to(mask_row.astype(F32), (CP, Z))
@@ -221,7 +250,7 @@
     for y in range(Y):
         for copy in dual_in[y]:
             copy.wait()
-    for y in range(Y):
+    def alone(y):
         fields = [diff_z(y), own[y] * STEP_DUAL]
         if y < Y - 1:
             fields.append(diff_y(y))
@@ -230,37 +259,66 @@
         sign(y, mm[1])
         if y < Y - 1:
             dual[1, y] = dual[1, y] + mm[2]
+    for y in range(Y // 2):
+        alone(y)
+
+    @pl.when(both(even, has_ym))
+    def _():
+        pl.semaphore_wait(ready, 1)
+        face_copy.start()
+    sent_a["my"] = Message(mown, my, ab, 5, to_ym, has_ym, has_yp)
+    sent_a["mx"] = Message(mown, mx, ab, 6, to_xm, has_xm, has_xp)
+    for y in range(Y // 2, Y):
+        alone(y)
 
     bb = (b_s, b_r)
-    sent_b = {}
+    sent_b = {
+        "hy": Message(hy_s.at[real, :], hy_r.at[real, :], bb, 8, to_yp, has_yp, has_ym, False),
+        "hyd": Message(hy_s.at[real, :], hyd_r.at[real, :], bb, 9, up_left, has_ul, has_dr, False),
+        "hx7": Message(hx_s.at[7, real, :], hx_r.at[7, real, :], bb, 12, to_xp, has_xp, has_xm, False),
+    }
+
+    def last_row():
+        sent_a[3].arrived()
+        pl.when(has_yp)(face_copy.wait_recv)
+        mm = lift(1, [diff_x(7), diff_y(7)])
+        shrink(7, dual[0, 7] + mm[0], dual[1, 7] + mm[1], dual[2, 7])
+        across, face = drop(1, [dual[1, 7], dual[0, 7]])
+        hy_s[...] = across * keep_y
+        hx_s[7] = face * keep_x
+        for key in ("hy", "hyd", "hx7"):
+            sent_b[key].go()
+
+    pl.when(far_above)(last_row)
     for p in range(4):
         ya, yb = 2 * p, 2 * p + 1
         two = pl.ds(ya, 2)
-        sent_a[p].arrived()
-        if yb == Y - 1:
-            sent_a["ey"].arrived()
-            mm = lift(p % 2, [diff_x(yb), diff_y(yb), diff_x(ya)])
-            shrink(yb, dual[0, yb] + mm[0], dual[1, yb] + mm[1], dual[2, yb])
-            hy_s[...] = drop(0, [dual[1, yb]])[0] * keep_y
-            sent_b["hy"] = Message(hy_s.at[real, :], hy_r.at[real, :], bb, 8, to_yp, has_yp, has_ym)
-            sent_b["hyd"] = Message(hy_s.at[real, :], hyd_r.at[real, :], bb, 9, up_left, has_ul, has_dr)
-            shrink(ya, dual[0, ya] + mm[2], dual[1, ya], dual[2, ya])
+        if p == 3:
+            pl.when(jnp.logical_not(far_above))(last_row)
+            mm = lift(0, [diff_x(6)])
+            shrink(6, dual[0, 6] + mm[0], dual[1, 6], dual[2, 6])
+            hx_s[6] = drop(0, [dual[0, 6]])[0] * keep_x
         else:
-            mm = lift(p % 2, [diff_x(ya), diff_x(yb)])
+            sent_a[p].arrived()
+            mm = lift(0, [diff_x(ya), diff_x(yb)])
             for y, part in ((ya, mm[0]), (yb, mm[1])):
                 shrink(y, dual[0, y] + part, dual[1, y], dual[2, y])
-        faces = drop(0, [dual[0, ya], dual[0, yb]])
-        harms = drop(1, [inner(ya), inner(yb)])
-        for y, face, harm in ((ya, faces[0], harms[0]), (yb, faces[1], harms[1])):
-            face = face * keep_x
-            hx_s[y] = face
-            u = advance(y, harm - face)
+            for y, face in zip((ya, yb), drop(0, [dual[0, ya], dual[0, yb]])):
+                hx_s[y] = face * keep_x
+        for y, harm in zip((ya, yb), drop(1, [inner(ya), inner(yb)])):
+            u = advance(y, harm - hx_s[y])
             up[y] = u
             ep_s[y] = 2.0 * u - cur[y]
         if p == 0:
             sent_b["epy"] = Message(ep_s.at[0, real, :], epy_r.at[real, :], bb, 10, to_ym, has_ym, has_yp)
+            @pl.when(both(even, has_dr, tail))
+            def _():
+                pl.semaphore_wait(ready_d, 1)
             sent_b["hxd"] = Message(hx_s.at[0, real, :], hxd_r.at[real, :], bb, 11, down_right, has_dr, has_ul)
-        sent_b["hx", p] = Message(hx_s.at[two, real, :], hx_r.at[two, real, :], bb, p, to_xp, has_xp, has_xm)
+        if p < 3:
+            sent_b["hx", p] = Message(hx_s.at[two, real, :], hx_r.at[two, real, :], bb, p, to_xp, has_xp, has_xm)
+        else:
+            sent_b["hx", p] = Message(hx_s.at[6, real, :], hx_r.at[6, real, :], bb, p, to_xp, has_xp, has_xm)
         sent_b["ep", p] = Message(ep_s.at[two, real, :], ep_r.at[two, real, :], bb, 4 + p, to_xm, has_xm, has_xp)
 
     sent_a["mx"].arrived()
@@ -268,6 +326,7 @@
     for y in range(Y):
         rdx[y] = recip(mx[y:y + 1, :])[0]
     rdy[...] = recip(my[0:1, :])[0]
+    pl.when(has_ym)(face_copy.wait_send)
     for key in sent_a:
         sent_a[key].left()
 
@@ -300,6 +359,22 @@
         for y in rows:
             sent_f["hx", y] = Message(hx2_s.at[y, real, :], hx2_r.at[y, real, :], ff, y, to_xp, has_xp, has_xm)
 
+    sent_f["hy"] = Message(hy2_s.at[real, :], hy2_r.at[real, :], ff, 8, to_yp, has_yp, has_ym, False)
+    sent_f["hx", 7] = Message(hx2_s.at[7, real, :], hx2_r.at[7, real, :], ff, 7, to_xp, has_xp, has_xm, False)
+
+    def last_again():
+        for key in ("hx7", ("ep", 3), "epy", "hxd"):
+            sent_b[key].arrived()
+        finish(7)
+        ey[...] = epy_r[...] - 2.0 * STEP_PRIMAL * rdy[...] * (hy_s[...] + hxd_r[...])
+        forward(7)
+        across, face = drop(1, [dual[1, 7], dual[0, 7]])
+        hy2_s[...] = across * keep_y
+        hx2_s[7] = face * keep_x
+        sent_f["hy"].go()
+        sent_f["hx", 7].go()
+
+    pl.when(far_below)(last_again)
     pair_here(0)
     pair_here(1)
     for y in (1, 2, 3):
@@ -313,19 +388,12 @@
     forward(3)
     forward(4)
     send_faces((3, 4))
-    pair_here(3)
-    sent_b["epy"].arrived()
-    sent_b["hxd"].arrived()
+    pl.when(jnp.logical_not(far_below))(last_again)
+    sent_b["hx", 3].arrived()
     finish(6)
-    finish(7)
-    ey[...] = epy_r[...] - 2.0 * STEP_PRIMAL * rdy[...] * (hy_s[...] + hxd_r[...])
-    forward(7)
-    hy2_s[...] = drop(0, [dual[1, Y - 1]])[0] * keep_y
-    sent_f["hy"] = Message(hy2_s.at[real, :], hy2_r.at[real, :], ff, 8, to_yp, has_yp, has_ym)
     forward(5)
     forward(6)
-    send_faces((6, 7))
-    send_faces((5,))
+    send_faces((5, 6))
     sent_b["hy"].arrived()
     sent_b["hyd"].arrived()
     finish(0)
@@ -340,7 +408,7 @@
     for key in sent_b:
         sent_b[key].left()
 
-    for y in (1, 2, 3, 4, 6, 7, 5, 0):
+    for y in (1, 2, 3, 4, 5, 6, 7, 0):
         sent_f["hx", y].arrived()
         face = hx2_r[y]
         if y == 0:
@@ -384,7 +452,8 @@
             pltpu.VMEM((NP, 256), BF16), pltpu.VMEM((2 * CP, 768), BF16),
             pltpu.VMEM((2, 256, 4 * Z), BF16), pltpu.VMEM((2, 768, 2 * Z), BF16),
             block, block, face, block, block, face, face, face, face, block, face, block, face,
-            dma((27,)), dma((Y, 4)), dma((7,)), dma((7,)), dma((12,)), dma((12,)), dma((9,)), dma((9,)),
+            dma((27,)), dma((Y, 4)), dma((7,)), dma((7,)), dma((13,)), dma((13,)), dma((9,)), dma((9,)),
+            pltpu.SemaphoreType.REGULAR, pltpu.SemaphoreType.REGULAR,
         ],
         compiler_params=pltpu.CompilerParams(collective_id=0, has_side_effects=True, vmem_limit_bytes=40 * 2**20),
         name="steps",

time: 31.1 us -> 29.7 us (0.955)
  Pallas kernels: 30.2 us -> 29 us
    pallas_call x1, Pallas kernels: 27.1 us -> 26 us  [per_device(): pl.pallas_call(main_kernel, out_shape=(pltpu.VMEM((4, Y, NP, Z), F32), pl...]
where the time goes in v3:
time: 29.7 us; the launch traced here: 29.6 us
  Pallas kernels  29 us (98%)
  between operations  0.64 us (2%)
    pallas_call x1, Pallas kernels, per_device(): pl.pallas_call(main_kernel, out_shape=(pltpu.VMEM((4, Y, NP, Z), F32), pl...  26 us
    pallas_call x1, Pallas kernels, per_device(): pl.pallas_call(write_kernel, out_shape=(jax.ShapeDtypeStruct((C, Y, Z), F...  3.04 us

profile of v3, /device:TPU:26, one launch (start us, length us, event | category | flops | bytes accessed | tf_op | source)
XLA Modules:
  0.0 29.6 jit_solution(4979423452954320800)
XLA Ops:
  0.6 26.0 %steps.1 = (f32[4,8,368,128]{3,2,1,0:T(8,128)S(1)}, f32[8,48,128]{2,1,0:T(8,128)S(1)}, f32[8,48,128]{2,1,0:T(8,128)S(1)}) custom-call(f32[45,8,128]{2,1,0:T(8,128)} %bitcast.22, f32[1,45]{1,0:T(1,128)} %bitcast.27, f32[45,362]{1,0:T(8,128)} %bitcast.25, s32[8,128]{1,0:T(8,128)} %bitcast.26, f32[45,8,128]{2,1,0:T(8,128)} %bitcast.23, f32[45,8,128]{2,1,0:T(8,128)} %bitcast.24, ...), custom_call_target="tpu_custom_call" | custom-call | tf_op jit(solution)/shard_map/steps/pallas_call | solution.py:443
  26.6 3.0 %write.1 = (f32[45,8,128]{2,1,0:T(8,128)}, f32[45,8,128]{2,1,0:T(8,128)}, f32[3,362,8,128]{3,2,1,0:T(8,128)}, f32[362,8,128]{2,1,0:T(8,128)}) custom-call(f32[4,8,368,128]{3,2,1,0:T(8,128)S(1)} %get-tuple-element.11.dual, f32[8,48,128]{2,1,0:T(8,128)S(1)} %get-tuple-element.12.cnew, f32[8,48,128]{2,1,0:T(8,128)S(1)} %get-tuple-element.13.enew), custom_call_target="tpu_custom_call" | custom-call | tf_op jit(solution)/shard_map/write/pallas_call | solution.py:464

commit v4 on v3

--- a/solution.py
+++ b/solution.py
@@ -394,17 +394,25 @@
     forward(5)
     forward(6)
     send_faces((5, 6))
+
+    def settle(p):
+        ya, yb = 2 * p, 2 * p + 1
+        for y, harm in zip((ya, yb), drop(p % 2, [inner(ya), inner(yb)])):
+            up[y] = advance(y, harm - hx2_s[y])
+
+    def settle_middle():
+        settle(1)
+        settle(2)
+    pl.when(jnp.logical_not(far_above))(settle_middle)
     sent_b["hy"].arrived()
     sent_b["hyd"].arrived()
     finish(0)
     forward(0)
     send_faces((0,))
 
-    for p in range(4):
-        ya, yb = 2 * p, 2 * p + 1
-        harms = drop(p % 2, [inner(ya), inner(yb)])
-        for y, harm in ((ya, harms[0]), (yb, harms[1])):
-            up[y] = advance(y, harm - hx2_s[y])
+    settle(0)
+    settle(3)
+    pl.when(far_above)(settle_middle)
     for key in sent_b:
         sent_b[key].left()
 

time: 29.7 us -> 30.3 us (1.020)
  the two profiles are of different devices: /device:TPU:26 before, /device:TPU:27 now
where the time goes in v4:
time: 30.3 us; the launch traced here: 30.2 us
  Pallas kernels  29.6 us (98%)
  between operations  0.64 us (2%)
    pallas_call x1, Pallas kernels, per_device(): pl.pallas_call(main_kernel, out_shape=(pltpu.VMEM((4, Y, NP, Z), F32), pl...  26.5 us
    pallas_call x1, Pallas kernels, per_device(): pl.pallas_call(write_kernel, out_shape=(jax.ShapeDtypeStruct((C, Y, Z), F...  3.04 us

profile of v4, /device:TPU:27, one launch (start us, length us, event | category | flops | bytes accessed | tf_op | source)
XLA Modules:
  0.0 30.2 jit_solution(2010039126488708455)
XLA Ops:
  0.6 26.5 %steps.1 = (f32[4,8,368,128]{3,2,1,0:T(8,128)S(1)}, f32[8,48,128]{2,1,0:T(8,128)S(1)}, f32[8,48,128]{2,1,0:T(8,128)S(1)}) custom-call(f32[45,8,128]{2,1,0:T(8,128)} %bitcast.22, f32[1,45]{1,0:T(1,128)} %bitcast.27, f32[45,362]{1,0:T(8,128)} %bitcast.25, s32[8,128]{1,0:T(8,128)} %bitcast.26, f32[45,8,128]{2,1,0:T(8,128)} %bitcast.23, f32[45,8,128]{2,1,0:T(8,128)} %bitcast.24, ...), custom_call_target="tpu_custom_call" | custom-call | tf_op jit(solution)/shard_map/steps/pallas_call | solution.py:451
  27.2 3.0 %write.1 = (f32[45,8,128]{2,1,0:T(8,128)}, f32[45,8,128]{2,1,0:T(8,128)}, f32[3,362,8,128]{3,2,1,0:T(8,128)}, f32[362,8,128]{2,1,0:T(8,128)}) custom-call(f32[4,8,368,128]{3,2,1,0:T(8,128)S(1)} %get-tuple-element.11.dual, f32[8,48,128]{2,1,0:T(8,128)S(1)} %get-tuple-element.12.cnew, f32[8,48,128]{2,1,0:T(8,128)S(1)} %get-tuple-element.13.enew), custom_call_target="tpu_custom_call" | custom-call | tf_op jit(solution)/shard_map/write/pallas_call | solution.py:472
